TPU v7x, 32 devices: a whole 2x2x4 slice. The times are simulated.
32 devices in a mesh: pts: 8 (over z, y), hrs: 4 (over x, core).
Axes of the slice: x: 2, y: 2, z: 4, core: 2. Of those that a mesh axis runs over, the one named last changes fastest.
Arguments:
- fields: float32 [512, 65536], P(('pts', 'hrs')), may hold values from -2000 to 2000, as said below
- probes: float32 [256, 512], replicated, may hold values from -0.25 to 0.25
Outputs:
- basis_rows: float32 [256, 65536], P(None, ('pts', 'hrs'))
- coeffs: float32 [256, 512], replicated
Inputs may be any that keep to these rules, and one draw needn't show every extreme that they name: `fields`: every hour and every grid point carries its own scale, and the values are real-valued and never all zero.
All inputs are finite; a program needn't handle non-finite values.
Results may differ from a plain program's by a relative error of at most 0.00017.
Values sent between devices are 32-bit elements; how exact they have to be, the bound alone decides.
A program may use at most 64 MiB of HBM per device.

v0:
```python
import jax
import jax.numpy as jnp
from jax import lax
from jax.sharding import PartitionSpec as P

highest = lax.Precision.HIGHEST


def contract_last(left, right):
    return lax.dot_general(
        left, right, (((1,), (1,)), ((), ())), precision=highest, preferred_element_type=jnp.float32
    )


def on_device(fields, probes):
    n_pts = lax.axis_size("pts")
    n_hrs = lax.axis_size("hrs")
    panels = lax.all_to_all(fields, ("pts", "hrs"), split_axis=1, concat_axis=0, tiled=True)
    n_points = panels.shape[1] * n_pts * n_hrs
    sketched = jnp.dot(probes, panels, precision=highest, preferred_element_type=jnp.float32)
    cross_sum = lax.psum(contract_last(sketched, panels) / n_points, ("pts", "hrs"))
    local_gram = contract_last(sketched, sketched) / n_points
    gram_sum = lax.psum(local_gram, ("pts", "hrs"))
    factor = jnp.linalg.cholesky(gram_sum)
    basis_rows = lax.linalg.triangular_solve(factor, sketched, left_side=True, lower=True)
    coeffs = lax.linalg.triangular_solve(factor, cross_sum, left_side=True, lower=True)
    return (basis_rows, coeffs)


def solution(mesh):
    return jax.shard_map(
        on_device,
        mesh=mesh,
        in_specs=(P(("pts", "hrs"), None), P()),
        out_specs=(P(None, ("pts", "hrs")), P()),
        check_vma=False,
    )
```

profile of v0, /device:TPU:0, one launch (start us, length us, event | category | flops | bytes accessed | tf_op | source)
XLA Modules:
  0.0 328.4 jit_solution(12238962326394786213)
XLA Ops:
  7.2 0.0 copy-start
  7.2 0.0 all-reduce.4.cloned.1.call-start
  7.2 2.5 copy.17
  9.7 100.7 %all_to_all.19 = f32[16,32,2048]{2,0,1:T(8,128)S(1)} all-to-all(f32[16,32,2048]{2,0,1:T(8,128)S(1)} %bitcast.50), channel_id=1, replica_groups=mesh['pts'=8,'hrs'=4] {'pts','hrs'}, dimensions={1} | all-to-all | bytes 8388608 | tf_op jit(solution)/shard_map/all_to_all | solution.py:18
  110.5 0.0 copy-done
  110.5 3.7 %fusion.13 = f32[256,2048]{1,0:T(8,128)S(1)} fusion(f32[256,512]{1,0:T(8,128)S(1)} %copy-done, f32[512,2048]{1,0:T(8,128)S(1)} %bitcast.48), kind=kOutput, calls=%fused_computation.38 | convolution fusion | flops 3221225472 | bytes 6815744 | tf_op jit(solution)/shard_map/dot_general | solution.py:20
  114.2 4.5 %convolution_multiply_fusion = f32[256,512]{1,0:T(8,128)} fusion(f32[256,2048]{1,0:T(8,128)S(1)} %fusion.13, f32[512,2048]{1,0:T(8,128)S(1)} %bitcast.49), kind=kOutput, calls=%fused_computation.5 | convolution fusion | flops 3221356544 | bytes 6815744 | tf_op jit(solution)/shard_map/dot_general | solution.py:10
  118.7 2.6 convolution_multiply_fusion.1
  121.3 0.0 all-reduce.4.cloned.1.call-update
  121.3 129.5 %all-reduce.4.cloned.1.call-done = (f32[256,256]{0,1:T(8,128)}, f32[256,512]{1,0:T(8,128)}) async-done(((f32[256,256]{0,1:T(8,128)}, f32[256,512]{1,0:T(8,128)}), (f32[256,256]{0,1:T(8,128)}, f32[256,512]{1,0:T(8,128)})) %all-reduce.4.cloned.1.call-update) | async-done | bytes 786448 | tf_op jit(solution)/shard_map/psum | solution.py:23
  250.9 1.1 copy.13
  252.0 1.0 fusion.4
  253.0 11.9 %cholesky.50 = f32[128,128]{1,0:T(8,128)S(1)} custom-call(f32[128,128]{1,0:T(8,128)S(1)} %cholesky.118), custom_call_target="Cholesky" | custom-call | tf_op jit(solution)/shard_map/jit(cholesky)/cholesky | solution.py:24
  264.9 9.8 %custom-call.16 = f32[1,128,128]{1,2,0:T(8,128)S(1)} custom-call(f32[1,128,128]{2,1,0:T(8,128)S(1)} %get-tuple-element.25), custom_call_target="InvertDiagBlocksLowerTriangular" | custom-call | tf_op jit(solution)/shard_map/jit(cholesky)/cholesky | solution.py:24
  274.7 0.2 constant_dynamic-update-slice_fusion.1
  274.9 0.3 convolution_subtract_fusion.2
  275.2 11.7 %cholesky.105 = f32[128,128]{1,0:T(8,128)S(1)} custom-call(f32[128,128]{1,0:T(8,128)S(1)} %convolution_subtract_fusion.2), custom_call_target="Cholesky" | custom-call | tf_op jit(solution)/shard_map/jit(cholesky)/cholesky | solution.py:24
  287.0 0.6 compare_reduce_fusion
  288.9 0.1 triangular_solve.72
  289.0 4.0 %while.1 = (s32[]{:T(128)}, f32[256,256]{1,0:T(8,128)S(1)}, s32[2,2]{1,0:T(2,128)S(1)}, f32[2,128,128]{2,1,0:T(8,128)S(1)}, s32[]{:T(128)}) while((s32[]{:T(128)}, f32[256,256]{1,0:T(8,128)S(1)}, s32[2,2]{1,0:T(2,128)S(1)}, f32[2,128,128]{2,1,0:T(8,128)S(1)}, s32[]{:T(128)}) %tuple.27), condition=%wide.while_cond, body=%wide.while_body.sunk | while | flops 2 | bytes 131181 | solution.py:25
  289.0 0.6 fusion.27
  289.6 1.4 bitcast_dynamic-update-slice_fusion.2
  291.0 0.6 fusion.27
  291.6 1.4 bitcast_dynamic-update-slice_fusion.2
  293.0 19.9 %custom-call.17 = f32[2,128,128]{1,2,0:T(8,128)S(1)} custom-call(f32[2,128,128]{2,1,0:T(8,128)S(1)} %get-tuple-element.9), custom_call_target="InvertDiagBlocksLowerTriangular" | custom-call | tf_op jit(solution)/shard_map/triangular_solve | solution.py:25
  312.9 1.1 fusion
  314.0 1.4 fusion.2
  315.3 1.3 convolution_subtract_fusion.1
  316.7 0.4 fusion.8
  317.1 0.8 pad_maximum_fusion.1
  317.9 1.0 convolution_subtract_fusion
  319.0 1.0 fusion.9
  320.0 1.5 pad_maximum_fusion
  (9 shorter events, 0.1 us)
Async XLA Ops:
  7.2 103.3 %copy-start = (f32[256,512]{1,0:T(8,128)S(1)}, f32[256,512]{1,0:T(8,128)}, u32[]{:S(2)}) copy-start(f32[256,512]{1,0:T(8,128)} %param.3) | copy-start | bytes 1572868
  7.2 243.7 %all-reduce.4.cloned.1.call-start = ((), (), s32[]{:S(2)}) async-start(), calls=%async_computation.1 | async-start | bytes 1572864 | tf_op jit(solution)/shard_map/psum | solution.py:23
Sparse Core Ops, SparseCore 0:
  121.4 129.3 all-reduce.3
where the time goes:
time: 329 us; the launch traced here: 328 us
  waiting for transfers between devices  130 us (40%)
  blocking collectives  101 us (31%)
  other arithmetic  57.4 us (17%)
  matrix products  17.5 us (5%)
  between operations  15.5 us (5%)
  local copies, waits for them, and re-layouts  7.64 us (2%)
    psum x1, waiting for transfers between devices, on_device(): gram_sum = lax.psum(local_gram, ('pts', 'hrs'))  130 us
    all_to_all x1, blocking collectives, on_device(): lax.all_to_all(fields, ('pts', 'hrs'), split_axis=1, concat_axis=0, tiled...  101 us
    another operation x6, other arithmetic, on_device(): factor = jnp.linalg.cholesky(gram_sum)  34.1 us
    another operation x4, other arithmetic, on_device(): lax.linalg.triangular_solve(factor, sketched, left_side=True, lower=True)  21.5 us
    dot_general x2, matrix products, contract_last(): lax.dot_general(left, right, (((1,), (1,)), ((), ())), precision=highest,...  7.09 us
  transfers between devices with their start and end apart: 1, of which 1 were waited for; matrix products, arithmetic and copies ran while one was open for 0% of the time, Pallas kernels for 0%

commit v1 on v0

--- a/solution.py
+++ b/solution.py
@@ -20,7 +20,7 @@
     sketched = jnp.dot(probes, panels, precision=highest, preferred_element_type=jnp.float32)
     cross_sum = lax.psum(contract_last(sketched, panels) / n_points, ("pts", "hrs"))
     local_gram = contract_last(sketched, sketched) / n_points
-    gram_sum = lax.psum(local_gram, ("pts", "hrs"))
+    gram_sum = jnp.sum(lax.all_gather(local_gram, ("pts", "hrs")), axis=0)
     factor = jnp.linalg.cholesky(gram_sum)
     basis_rows = lax.linalg.triangular_solve(factor, sketched, left_side=True, lower=True)
     coeffs = lax.linalg.triangular_solve(factor, cross_sum, left_side=True, lower=True)

time: 329 us -> 342 us (1.040)
  waiting for transfers between devices: 130 us -> 138 us
    all_gather x0 -> x1, waiting for transfers between devices: none -> 69.3 us  [on_device(): gram_sum = jnp.sum(lax.all_gather(local_gram, ('pts', 'hrs')), axis=0)]
    psum x1, waiting for transfers between devices: 130 us -> 68.4 us  [on_device(): lax.psum(contract_last(sketched, panels) / n_points, ('pts', 'hrs'))]
    reduce_sum x0 -> x1, other arithmetic: none -> 3.93 us  [on_device(): gram_sum = jnp.sum(lax.all_gather(local_gram, ('pts', 'hrs')), axis=0)]
  transfers between devices with their start and end apart: 1 -> 2, of which waited for: 1 -> 2; matrix products, arithmetic and copies ran while one was open for 0% -> 21% of each run, Pallas kernels for 0% -> 0%
where the time goes in v1:
time: 342 us
  waiting for transfers between devices  138 us (40%)
  blocking collectives  101 us (30%)
  other arithmetic  60.2 us (18%)
  matrix products  20.7 us (6%)
  between operations  15.5 us (5%)
  local copies, waits for them, and re-layouts  6.69 us (2%)
    all_to_all x1, blocking collectives, on_device(): lax.all_to_all(fields, ('pts', 'hrs'), split_axis=1, concat_axis=0, tiled...  101 us
    all_gather x1, waiting for transfers between devices, on_device(): gram_sum = jnp.sum(lax.all_gather(local_gram, ('pts', 'hrs')), axis=0)  69.3 us
    psum x1, waiting for transfers between devices, on_device(): lax.psum(contract_last(sketched, panels) / n_points, ('pts', 'hrs'))  68.4 us
    another operation x6, other arithmetic, on_device(): factor = jnp.linalg.cholesky(gram_sum)  34.2 us
    another operation x4, other arithmetic, on_device(): lax.linalg.triangular_solve(factor, sketched, left_side=True, lower=True)  21.2 us
    dot_general x2, matrix products, contract_last(): lax.dot_general(left, right, (((1,), (1,)), ((), ())), precision=highest,...  9.24 us
  transfers between devices with their start and end apart: 2, of which 2 were waited for; matrix products, arithmetic and copies ran while one was open for 21% of the time, Pallas kernels for 0%

profile of v1, /device:TPU:0, one launch (start us, length us, event | category | flops | bytes accessed | tf_op | source)
XLA Modules:
  0.0 341.9 jit_solution(9663236041237582199)
XLA Ops:
  7.2 0.0 copy-start
  7.2 0.0 all-gather.3.cloned.1.call-start
  7.2 2.5 copy.12
  9.7 100.7 %all_to_all.19 = f32[16,32,2048]{2,0,1:T(8,128)S(1)} all-to-all(f32[16,32,2048]{2,0,1:T(8,128)S(1)} %bitcast.51), channel_id=1, replica_groups=mesh['pts'=8,'hrs'=4] {'pts','hrs'}, dimensions={1} | all-to-all | bytes 8388608 | tf_op jit(solution)/shard_map/all_to_all | solution.py:18
  110.5 0.0 copy-start.1
  110.5 0.0 copy-done
  110.5 3.7 %fusion.13 = f32[256,2048]{1,0:T(8,128)S(1)} fusion(f32[256,512]{1,0:T(8,128)S(1)} %copy-done, f32[512,2048]{1,0:T(8,128)S(1)} %bitcast.49), kind=kOutput, calls=%fused_computation.38 | convolution fusion | flops 3221225472 | bytes 6815744 | tf_op jit(solution)/shard_map/dot_general | solution.py:20
  114.2 0.0 copy-done.1
  114.2 2.6 convolution_multiply_fusion.1
  116.8 0.0 all-gather.3.cloned.1.call-update
  116.8 0.2 all-reduce.3.cloned.1.call-start
  117.1 6.7 %convolution_multiply_fusion = f32[256,512]{1,0:T(8,128)} fusion(f32[256,2048]{1,0:T(8,128)S(1)} %fusion.13, f32[512,2048]{1,0:T(8,128)} %bitcast.50), kind=kOutput, calls=%fused_computation.5 | convolution fusion | flops 3221356544 | bytes 6815744 | tf_op jit(solution)/shard_map/dot_general | solution.py:10
  123.7 0.0 all-reduce.3.cloned.1.call-update
  123.7 69.3 %all-gather.3.cloned.1.call-done = f32[8192,256]{1,0:T(8,128)} async-done(((f32[256,256]{1,0:T(8,128)}), f32[8192,256]{1,0:T(8,128)}) %all-gather.3.cloned.1.call-update) | async-done | bytes 8388624 | tf_op jit(solution)/shard_map/all_gather | solution.py:23
  193.1 3.9 %reduce_sum.9 = f32[256,256]{1,0:T(8,128)S(1)} reduce(f32[32,256,256]{2,1,0:T(8,128)} %bitcast.52, f32[]{:T(128)} %constant.83.clone.1), dimensions={0}, to_apply=%region_0.0 | reduce | flops 2031616 | bytes 8650756 | tf_op jit(solution)/shard_map/reduce_sum | solution.py:23
  197.0 0.1 copy.9
  197.2 11.7 %cholesky.50 = f32[128,128]{1,0:T(8,128)S(1)} custom-call(f32[128,128]{1,0:T(8,128)S(1)} %cholesky.118), custom_call_target="Cholesky" | custom-call | tf_op jit(solution)/shard_map/jit(cholesky)/cholesky | solution.py:24
  209.0 9.8 %custom-call.16 = f32[1,128,128]{1,2,0:T(8,128)S(1)} custom-call(f32[1,128,128]{2,1,0:T(8,128)S(1)} %get-tuple-element.23), custom_call_target="InvertDiagBlocksLowerTriangular" | custom-call | tf_op jit(solution)/shard_map/jit(cholesky)/cholesky | solution.py:24
  218.8 0.2 constant_dynamic-update-slice_fusion.1
  219.0 0.3 convolution_subtract_fusion.2
  219.3 11.9 %cholesky.105 = f32[128,128]{1,0:T(8,128)S(1)} custom-call(f32[128,128]{1,0:T(8,128)S(1)} %convolution_subtract_fusion.2), custom_call_target="Cholesky" | custom-call | tf_op jit(solution)/shard_map/jit(cholesky)/cholesky | solution.py:24
  231.2 0.7 compare_reduce_fusion
  233.2 0.1 triangular_solve.72
  233.3 4.0 %while.1 = (s32[]{:T(128)}, f32[256,256]{1,0:T(8,128)S(1)}, s32[2,2]{1,0:T(2,128)S(1)}, f32[2,128,128]{2,1,0:T(8,128)S(1)}, s32[]{:T(128)}) while((s32[]{:T(128)}, f32[256,256]{1,0:T(8,128)S(1)}, s32[2,2]{1,0:T(2,128)S(1)}, f32[2,128,128]{2,1,0:T(8,128)S(1)}, s32[]{:T(128)}) %tuple.27), condition=%wide.while_cond, body=%wide.while_body.sunk | while | flops 2 | bytes 131189 | solution.py:25
  233.3 0.6 fusion.27
  233.9 1.4 bitcast_dynamic-update-slice_fusion.2
  235.3 0.6 fusion.27
  235.9 1.4 bitcast_dynamic-update-slice_fusion.2
  237.3 19.7 %custom-call.17 = f32[2,128,128]{1,2,0:T(8,128)S(1)} custom-call(f32[2,128,128]{2,1,0:T(8,128)S(1)} %get-tuple-element.9), custom_call_target="InvertDiagBlocksLowerTriangular" | custom-call | tf_op jit(solution)/shard_map/triangular_solve | solution.py:25
  256.9 2.0 fusion
  259.0 68.4 %all-reduce.3.cloned.1.call-done = f32[256,512]{1,0:T(8,128)} async-done(((f32[256,512]{1,0:T(8,128)}), f32[256,512]{1,0:T(8,128)}) %all-reduce.3.cloned.1.call-update) | async-done | bytes 524304 | tf_op jit(solution)/shard_map/psum | solution.py:21
  327.4 0.0 copy-start.2
  327.4 1.5 fusion.2
  328.9 1.3 convolution_subtract_fusion.1
  330.2 0.4 fusion.8
  330.6 0.8 pad_maximum_fusion.1
  331.5 0.0 copy-done.2
  331.5 1.0 convolution_subtract_fusion
  332.5 1.1 fusion.9
  333.5 1.5 pad_maximum_fusion
  (10 shorter events, 0.2 us)
Async XLA Ops:
  7.2 103.3 %copy-start = (f32[256,512]{1,0:T(8,128)S(1)}, f32[256,512]{1,0:T(8,128)}, u32[]{:S(2)}) copy-start(f32[256,512]{1,0:T(8,128)} %param.3) | copy-start | bytes 1572868
  7.2 185.9 %all-gather.3.cloned.1.call-start = ((), (), s32[]{:S(2)}) async-start(), calls=%async_computation.2 | async-start | bytes 8650752 | tf_op jit(solution)/shard_map/all_gather | solution.py:23
  110.5 3.7 %copy-start.1 = (f32[16,32,2048]{2,0,1:T(8,128)}, f32[16,32,2048]{2,0,1:T(8,128)S(1)}, u32[]{:S(2)}) copy-start(f32[16,32,2048]{2,0,1:T(8,128)S(1)} %all_to_all.19) | copy-start | bytes 12582916
  116.8 210.6 %all-reduce.3.cloned.1.call-start = ((), (), s32[]{:S(2)}) async-start(), calls=%async_computation.1 | async-start | bytes 1048576 | tf_op jit(solution)/shard_map/psum | solution.py:21
  327.4 4.1 %copy-start.2 = (f32[128,2048]{1,0:T(8,128)S(1)}, f32[128,2048]{1,0:T(8,128)}, u32[]{:S(2)}) copy-start(f32[128,2048]{1,0:T(8,128)} %fusion) | copy-start | bytes 3145732
Sparse Core Ops, SparseCore 0:
  116.9 76.0 all-gather.2
  198.9 128.4 all-reduce.2
